TPU v7x, 32 devices: a whole 2x2x4 slice. The times are simulated.
32 devices in a mesh: gx: 2 (over y), gy: 16 (over z, x, core).
Axes of the slice: x: 2, y: 2, z: 4, core: 2. Of those that a mesh axis runs over, the one named last changes fastest.
Arguments:
- basis_mats: float32 [12, 275, 275], replicated, may hold values from -8 to 8.5, as said below
- coeffs: float32 [512, 12], P(('gx', 'gy')), may hold values from 0.5 to 2
- element_loads: float32 [512, 275], P(('gx', 'gy')), may hold values from -18 to 18
- elem_faces: int32 [512, 6], P(('gx', 'gy')), may hold values from 0 to 71, as said below
- orient_codes: int32 [512, 6], P(('gx', 'gy')), may hold values from 0 to 7
- shared_owned: int32 [32, 2, 4], P(('gx', 'gy')), may hold values from 0 to 63, as said below
- shared_remote: int32 [32, 2, 4], P(('gx', 'gy')), may hold values from 0 to 7, as said below
- lower_peers: int32 [32, 2], P(('gx', 'gy')), may hold values from 0 to 31, as said below
- upper_peers: int32 [32, 2], P(('gx', 'gy')), may hold values from 0 to 31, as said below
Outputs:
- trace: float32 [25, 2048], P(None, ('gx', 'gy'))
- residual: float32 [25, 2048], P(None, ('gx', 'gy'))
Inputs may be any that keep to these rules, and one draw needn't show every extreme that they name: `basis_mats`: each matrix is symmetric with every eigenvalue at least 0.5. `elem_faces`: an entry below 64 is a face slot that the element's device owns; an entry 64 + r is that device's remote slot r. Every owned slot of a device is named by one or two of its element faces, every remote slot by exactly one. `shared_owned`: row (d, i) lists 4 distinct owned slots of device d, in message order, that device lower_peers[d, i] uses; the two rows of a device are disjoint. `shared_remote`: row (d, i) lists remote slots of device d in message order: its k-th entry is the face that device upper_peers[d, i] lists k-th in its row i of shared_owned. The two rows of a device together hold each of its 8 remote slots once. upper_peers[lower_peers[d, i], i] = d for every device d and i; the two entries of a row differ. Peers are arbitrary device numbers. lower_peers[upper_peers[d, i], i] = d for every device d and i; the two entries of a row differ; each column is a permutation of the devices. Peers are arbitrary device numbers.
All inputs are finite; a program needn't handle non-finite values.
Results may differ from a plain program's by a relative error of at most 0.0003.
Values sent between devices are 32-bit elements; how exact they have to be, the bound alone decides.
A program may use at most 128 MiB of HBM per device.

v0:
```python
import math
import jax
import jax.numpy as jnp
import numpy as np
from jax import lax
from jax.sharding import PartitionSpec as P

SIDE = 5
FACE_DOFS = 25
CELL_DOFS = 125
TRACE_DOFS = 150
ITERS = 4
FACE_DEV = 64
SHARED = 4
REMOTE = 8
full_precision = lax.Precision.HIGHEST


def orient_table():
    edge_nodes = SIDE
    codes_table = np.zeros((8, edge_nodes * edge_nodes), np.int32)
    for code_index in range(8):
        for first_axis in range(edge_nodes):
            for second_axis in range(edge_nodes):
                if code_index & 1:
                    first_new, second_new = (second_axis, first_axis)
                else:
                    first_new, second_new = (first_axis, second_axis)
                if code_index & 2:
                    first_new = edge_nodes - 1 - first_new
                if code_index & 4:
                    second_new = edge_nodes - 1 - second_new
                codes_table[code_index, first_axis * edge_nodes + second_axis] = (
                    first_new * edge_nodes + second_new
                )
    return codes_table


def permute_mats():
    codes_table = orient_table()
    matrices = np.zeros((8, FACE_DOFS, FACE_DOFS), np.float32)
    for code_index in range(8):
        for position in range(FACE_DOFS):
            matrices[code_index, position, codes_table[code_index, position]] = 1.0
    return matrices


def condense(coeffs, element_loads, basis_mats):
    element_mats = jnp.einsum("ek,kab->eab", coeffs, basis_mats, precision=full_precision)
    inner_block = element_mats[:, :CELL_DOFS, :CELL_DOFS]
    coupling = element_mats[:, :CELL_DOFS, CELL_DOFS:]
    outer_block = element_mats[:, CELL_DOFS:, CELL_DOFS:]
    factor = jnp.linalg.cholesky(inner_block)
    solved = jax.scipy.linalg.solve_triangular(factor, coupling, lower=True)
    source = jax.scipy.linalg.solve_triangular(
        factor, element_loads[:, :CELL_DOFS, None], lower=True
    )[:, :, 0]
    schur_part = outer_block - jnp.einsum("eib,eic->ebc", solved, solved, precision=full_precision)
    load_trace = element_loads[:, CELL_DOFS:] - jnp.einsum(
        "eib,ei->eb", solved, source, precision=full_precision
    )
    return (schur_part, load_trace)


def condense_blocks(coeffs, element_loads, basis_mats):
    elem_count = coeffs.shape[0]
    block_rows = math.gcd(elem_count, 16)
    grouped = (
        coeffs.reshape(-1, block_rows, coeffs.shape[1]),
        element_loads.reshape(-1, block_rows, element_loads.shape[1]),
    )
    schur_part, load_trace = lax.map(
        lambda pieces: condense(pieces[0], pieces[1], basis_mats), grouped
    )
    return (
        schur_part.reshape(elem_count, TRACE_DOFS, TRACE_DOFS),
        load_trace.reshape(elem_count, TRACE_DOFS),
    )


def pick_columns(fields, columns):
    picked = fields[:, :, columns]
    return jnp.moveaxis(picked, 2, 0).reshape(2, -1)


def place_rows(fields, columns, arrived):
    shaped = jnp.moveaxis(arrived.reshape(2, fields.shape[0], FACE_DOFS, SHARED), 0, 2)
    return fields.at[:, :, columns].add(shaped)


def owned_dot(first, second):
    return jnp.sum(first * second)


def on_device(
    basis_mats,
    coeffs,
    element_loads,
    elem_faces,
    orient_codes,
    shared_owned,
    shared_remote,
    lower_peers,
    upper_peers,
):
    elem_count = coeffs.shape[0]
    extent = FACE_DEV + REMOTE
    size_outer = lax.axis_size("gx")
    size_inner = lax.axis_size("gy")
    devices = size_outer * size_inner
    schur_blocks, load_trace = condense_blocks(coeffs, element_loads, basis_mats)
    choose = (orient_codes[:, :, None] == jnp.arange(8, dtype=jnp.int32)[None, None, :]).astype(
        jnp.float32
    )
    permute = jnp.einsum(
        "ejo,oqp->ejqp", choose, jnp.asarray(permute_mats()), precision=full_precision
    )
    incidence = (
        elem_faces.reshape(-1)[:, None] == jnp.arange(extent, dtype=jnp.int32)[None, :]
    ).astype(jnp.float32)
    owned_lists = shared_owned[0]
    remote_lists = FACE_DEV + shared_remote[0]
    lower_ids = lower_peers[0]
    upper_ids = upper_peers[0]

    def spread(field_values):
        gathered = jnp.dot(incidence, field_values.T, precision=full_precision).reshape(
            elem_count, 6, FACE_DOFS
        )
        return jnp.einsum("ejqp,ejp->ejq", permute, gathered, precision=full_precision).reshape(
            elem_count, TRACE_DOFS
        )

    def collect(element_values):
        shaped = element_values.reshape(elem_count, 6, FACE_DOFS)
        placed = jnp.einsum("ejqp,ejq->ejp", permute, shaped, precision=full_precision)
        return jnp.dot(
            placed.reshape(elem_count * 6, FACE_DOFS).T, incidence, precision=full_precision
        )

    def apply_blocks(field_values):
        return collect(
            jnp.einsum("ekl,el->ek", schur_blocks, spread(field_values), precision=full_precision)
        )

    fields = jnp.stack([collect(load_trace), collect(jnp.diagonal(schur_blocks, axis1=1, axis2=2))])

    def upward_bucket(partial_value):
        outgoing = pick_columns(partial_value, remote_lists)
        bucket = jnp.zeros((devices, outgoing.shape[1]), jnp.float32).at[upper_ids].set(outgoing)
        return bucket.reshape(size_outer, size_inner, -1)

    def upward_settle(partial_value, arrived):
        incoming = arrived.reshape(devices, -1)[lower_ids]
        return place_rows(partial_value[:, :, :FACE_DEV], owned_lists, incoming)

    def downward_bucket(values):
        outgoing = pick_columns(values[None], owned_lists)
        bucket = jnp.zeros((devices, outgoing.shape[1]), jnp.float32).at[lower_ids].set(outgoing)
        return bucket.reshape(size_outer, size_inner, -1)

    def downward_settle(values, arrived):
        incoming = arrived.reshape(devices, -1)[upper_ids]
        remote = place_rows(
            jnp.zeros((1, FACE_DOFS, REMOTE), jnp.float32), shared_remote[0], incoming
        )
        return jnp.concatenate([values, remote[0]], axis=1)

    arrived = lax.all_to_all(
        lax.all_to_all(upward_bucket(fields), "gx", split_axis=0, concat_axis=0, tiled=True),
        "gy",
        split_axis=1,
        concat_axis=1,
        tiled=True,
    )
    settled = upward_settle(fields, arrived)

    def operate(values):
        fetched = lax.all_to_all(
            lax.all_to_all(downward_bucket(values), "gx", split_axis=0, concat_axis=0, tiled=True),
            "gy",
            split_axis=1,
            concat_axis=1,
            tiled=True,
        )
        partial_value = apply_blocks(downward_settle(values, fetched))[None]
        returned = lax.all_to_all(
            lax.all_to_all(
                upward_bucket(partial_value), "gx", split_axis=0, concat_axis=0, tiled=True
            ),
            "gy",
            split_axis=1,
            concat_axis=1,
            tiled=True,
        )
        return upward_settle(partial_value, returned)[0]

    rhs_faces = settled[0]
    diag_faces = settled[1]

    def pair_total(residual, precond, mapped):
        return lax.psum((owned_dot(residual, precond), owned_dot(precond, mapped)), ("gx", "gy"))

    trace = jnp.zeros_like(rhs_faces)
    residual = rhs_faces
    precond = residual / diag_faces
    mapped = operate(precond)
    rz_now, curve_sum = pair_total(residual, precond, mapped)
    step_size = rz_now / curve_sum
    direction = precond
    direction_image = mapped
    for iteration in range(ITERS):
        trace = trace + step_size * direction
        residual = residual - step_size * direction_image
        if iteration + 1 < ITERS:
            precond = residual / diag_faces
            mapped = operate(precond)
            rz_next, curve_sum = pair_total(residual, precond, mapped)
            ratio_next = rz_next / rz_now
            step_size = rz_next / (curve_sum - ratio_next * rz_next / step_size)
            direction = precond + ratio_next * direction
            direction_image = mapped + ratio_next * direction_image
            rz_now = rz_next
    return (trace, residual)


def solution(mesh):
    placed = (
        P(),
        P(("gx", "gy"), None),
        P(("gx", "gy"), None),
        P(("gx", "gy"), None),
        P(("gx", "gy"), None),
        P(("gx", "gy"), None, None),
        P(("gx", "gy"), None, None),
        P(("gx", "gy"), None),
        P(("gx", "gy"), None),
    )
    return jax.shard_map(
        on_device,
        mesh=mesh,
        in_specs=placed,
        out_specs=(P(None, ("gx", "gy")), P(None, ("gx", "gy"))),
        check_vma=False,
    )
```

profile of v0, /device:TPU:0, one launch (start us, length us, event | category | flops | bytes accessed | tf_op | source)
XLA Modules:
  0.0 803.4 jit_solution(2315458276905869473)
XLA Ops:
  1.3 9.7 %fusion = f32[16,275,275]{2,0,1:T(8,128)S(1)} fusion(f32[12,275,275]{2,1,0:T(8,128)} %param.10, f32[16,12]{1,0:T(8,128)S(1)} %copy-done), kind=kOutput, calls=%fused_computation.37 | convolution fusion | flops 174240000 | bytes 8470768 | tf_op jit(solution)/shard_map/while/body/eval_jaxpr/ek,kab->eab/dot_general | solution.py:49
  16.7 183.1 %custom-call.13 = f32[16,125,125]{2,1,0:T(8,128)S(1)} custom-call(f32[16,125,125]{2,1,0:T(8,128)S(1)} %fusion.20), custom_call_target="Cholesky" | custom-call | tf_op jit(solution)/shard_map/while/body/eval_jaxpr/jit(cholesky)/cholesky | solution.py:53
  200.3 154.0 %custom-call.14 = f32[16,1,125,125]{2,3,1,0:T(8,128)S(1)} custom-call(f32[16,1,125,125]{3,2,1,0:T(8,128)S(1)} %select_bitcast_fusion), custom_call_target="InvertDiagBlocksLowerTriangular" | custom-call | tf_op jit(solution)/shard_map/while/body/eval_jaxpr/jit(_solve_triangular)/vmap()/triangular_solve | solution.py:54
  377.6 6.7 copy.285
  405.9 6.4 all-to-all-start.1
  412.4 6.5 all-to-all-done.1
  422.0 6.2 all_to_all.90
  432.5 6.3 all-to-all-done.3
  464.7 6.4 all-to-all-done.5
  473.1 38.3 %all-reduce.3 = (f32[]{:T(128)}, f32[]{:T(128)}) all-reduce(f32[]{:T(128)} %get-tuple-element.39, f32[]{:T(128)} %get-tuple-element.38), channel_id=1, replica_groups=mesh['gx'=2,'gy'=16] {'gx','gy'}, use_global_device_ids=true, to_apply=%region_5.6 | all-reduce | flops 2 | bytes 16 | tf_op jit(solution)/shard_map/psum | solution.py:202
  514.2 7.4 all_to_all.92
  525.8 6.4 all-to-all-done.7
  548.0 6.2 all_to_all.93
  558.4 6.4 all-to-all-done.9
  566.8 38.3 %all-reduce.2 = (f32[]{:T(128)}, f32[]{:T(128)}) all-reduce(f32[]{:T(128)} %get-tuple-element.37, f32[]{:T(128)} %get-tuple-element.36), channel_id=1, replica_groups=mesh['gx'=2,'gy'=16] {'gx','gy'}, use_global_device_ids=true, to_apply=%region_13.14 | all-reduce | flops 2 | bytes 16 | tf_op jit(solution)/shard_map/psum | solution.py:202
  611.0 7.4 all_to_all.94
  622.7 6.4 all-to-all-done.11
  644.6 6.2 all_to_all.95
  655.0 6.4 all-to-all-done.13
  663.4 38.3 %all-reduce.1 = (f32[]{:T(128)}, f32[]{:T(128)}) all-reduce(f32[]{:T(128)} %get-tuple-element.35, f32[]{:T(128)} %get-tuple-element.34), channel_id=1, replica_groups=mesh['gx'=2,'gy'=16] {'gx','gy'}, use_global_device_ids=true, to_apply=%region_21.22 | all-reduce | flops 2 | bytes 16 | tf_op jit(solution)/shard_map/psum | solution.py:202
  707.2 7.4 all_to_all.96
  718.8 6.4 all-to-all-done.15
  751.2 6.4 all-to-all-done.17
  759.7 38.4 %all-reduce = (f32[]{:T(128)}, f32[]{:T(128)}) all-reduce(f32[]{:T(128)} %get-tuple-element.33, f32[]{:T(128)} %get-tuple-element.32), channel_id=1, replica_groups=mesh['gx'=2,'gy'=16] {'gx','gy'}, use_global_device_ids=true, to_apply=%region_29.30 | all-reduce | flops 2 | bytes 16 | tf_op jit(solution)/shard_map/psum | solution.py:202
  (255 shorter events, 176.7 us)
Async XLA Ops:
  0.6 0.7 copy-start
  11.1 2.8 copy-start.2
  354.2 5.9 slice-start
  361.2 5.6 copy-start.4
  361.2 5.9 copy-start.3
  361.2 5.9 copy-start.5
  370.9 2.7 copy-start.1
  370.9 2.6 copy-start.6
  384.2 10.8 %copy-start.7 = (s32[1,2,4]{2,1,0:T(2,128)S(1)}, s32[1,2,4]{2,1,0:T(2,128)}, u32[]{:S(2)}) copy-start(s32[1,2,4]{2,1,0:T(2,128)} %param.16) | copy-start | bytes 100
  384.2 11.7 %copy-start.9 = (s32[1,2]{1,0:T(1,128)S(1)}, s32[1,2]{1,0:T(1,128)}, u32[]{:S(2)}) copy-start(s32[1,2]{1,0:T(1,128)} %param.18) | copy-start | bytes 28
  384.2 17.1 %copy-start.10 = (s32[1,2]{1,0:T(1,128)S(1)}, s32[1,2]{1,0:T(1,128)}, u32[]{:S(2)}) copy-start(s32[1,2]{1,0:T(1,128)} %param.17) | copy-start | bytes 28
  384.2 17.1 %copy-start.8 = (s32[1,2,4]{2,1,0:T(2,128)S(1)}, s32[1,2,4]{2,1,0:T(2,128)}, u32[]{:S(2)}) copy-start(s32[1,2,4]{2,1,0:T(2,128)} %param.15) | copy-start | bytes 100
  397.1 8.2 %all-to-all-start = ((f32[2,16,200]{2,1,0:T(8,128)}), f32[2,16,200]{2,1,0:T(8,128)S(1)}, u32[]{:S(2)}, u32[]{:S(2)}) async-start(f32[2,16,200]{2,1,0:T(8,128)} %bitcast.26), calls=%async_computation | async-start | bytes 65536 | tf_op jit(solution)/shard_map/all_to_all | solution.py:170
  405.9 13.0 %all-to-all-start.1 = ((f32[2,16,200]{2,0,1:T(2,128)}), f32[2,16,200]{2,0,1:T(2,128)S(1)}, u32[]{:S(2)}, u32[]{:S(2)}) async-start(f32[2,16,200]{2,0,1:T(2,128)} %copy.290), calls=%async_computation.1 | async-start | bytes 65536 | tf_op jit(solution)/shard_map/all_to_all | solution.py:169
  428.8 10.0 %all-to-all-start.3 = ((f32[2,16,100]{2,0,1:T(2,128)}), f32[2,16,100]{2,0,1:T(2,128)S(1)}, u32[]{:S(2)}, u32[]{:S(2)}) async-start(f32[2,16,100]{2,0,1:T(2,128)} %copy.298), calls=%async_computation.3 | async-start | bytes 32768 | tf_op jit(solution)/shard_map/all_to_all | solution.py:179
  461.1 10.0 %all-to-all-start.5 = ((f32[2,16,100]{2,0,1:T(2,128)}), f32[2,16,100]{2,0,1:T(2,128)S(1)}, u32[]{:S(2)}, u32[]{:S(2)}) async-start(f32[2,16,100]{2,0,1:T(2,128)} %copy.306), calls=%async_computation.5 | async-start | bytes 32768 | tf_op jit(solution)/shard_map/all_to_all | solution.py:187
  522.2 10.1 %all-to-all-start.7 = ((f32[2,16,100]{2,0,1:T(2,128)}), f32[2,16,100]{2,0,1:T(2,128)S(1)}, u32[]{:S(2)}, u32[]{:S(2)}) async-start(f32[2,16,100]{2,0,1:T(2,128)} %copy.312), calls=%async_computation.7 | async-start | bytes 32768 | tf_op jit(solution)/shard_map/all_to_all | solution.py:179
  554.8 10.0 %all-to-all-start.9 = ((f32[2,16,100]{2,0,1:T(2,128)}), f32[2,16,100]{2,0,1:T(2,128)S(1)}, u32[]{:S(2)}, u32[]{:S(2)}) async-start(f32[2,16,100]{2,0,1:T(2,128)} %copy.320), calls=%async_computation.9 | async-start | bytes 32768 | tf_op jit(solution)/shard_map/all_to_all | solution.py:187
  619.1 10.0 %all-to-all-start.11 = ((f32[2,16,100]{2,0,1:T(2,128)}), f32[2,16,100]{2,0,1:T(2,128)S(1)}, u32[]{:S(2)}, u32[]{:S(2)}) async-start(f32[2,16,100]{2,0,1:T(2,128)} %copy.326), calls=%async_computation.11 | async-start | bytes 32768 | tf_op jit(solution)/shard_map/all_to_all | solution.py:179
  651.4 10.0 %all-to-all-start.13 = ((f32[2,16,100]{2,0,1:T(2,128)}), f32[2,16,100]{2,0,1:T(2,128)S(1)}, u32[]{:S(2)}, u32[]{:S(2)}) async-start(f32[2,16,100]{2,0,1:T(2,128)} %copy.334), calls=%async_computation.13 | async-start | bytes 32768 | tf_op jit(solution)/shard_map/all_to_all | solution.py:187
  715.2 10.1 %all-to-all-start.15 = ((f32[2,16,100]{2,0,1:T(2,128)}), f32[2,16,100]{2,0,1:T(2,128)S(1)}, u32[]{:S(2)}, u32[]{:S(2)}) async-start(f32[2,16,100]{2,0,1:T(2,128)} %copy.340), calls=%async_computation.15 | async-start | bytes 32768 | tf_op jit(solution)/shard_map/all_to_all | solution.py:179
  747.6 10.0 %all-to-all-start.17 = ((f32[2,16,100]{2,0,1:T(2,128)}), f32[2,16,100]{2,0,1:T(2,128)S(1)}, u32[]{:S(2)}, u32[]{:S(2)}) async-start(f32[2,16,100]{2,0,1:T(2,128)} %copy.348), calls=%async_computation.17 | async-start | bytes 32768 | tf_op jit(solution)/shard_map/all_to_all | solution.py:187
where the time goes:
time: 814 us; the launch traced here: 803 us
  other arithmetic  352 us (43%)
  blocking collectives  207 us (25%)
  matrix products  79.3 us (10%)
  waiting for transfers between devices  61.3 us (8%)
  local copies, waits for them, and re-layouts  50.7 us (6%)
  starting transfers between devices  38.8 us (5%)
  between operations  15.2 us (2%)
    another operation x4, other arithmetic, condense(): factor = jnp.linalg.cholesky(inner_block)  183 us
    another operation x3, other arithmetic, condense(): solved = jax.scipy.linalg.solve_triangular(factor, coupling, lower=True)  154 us
    psum x4, blocking collectives, pair_total(): lax.psum((owned_dot(residual, precond), owned_dot(precond, mapped)), ('gx...  153 us
    all_to_all x4, blocking collectives, operate(): lax.all_to_all(downward_bucket(values), 'gx', split_axis=0, concat_axis=0...  28.4 us
    all_to_all x4, waiting for transfers between devices, operate(): lax.all_to_all(lax.all_to_all(downward_bucket(values), 'gx', split_axis=0...  25.5 us
    all_to_all x4, waiting for transfers between devices, operate(): lax.all_to_all(lax.all_to_all(upward_bucket(partial_value), 'gx', split_a...  25.4 us
    all_to_all x4, blocking collectives, operate(): lax.all_to_all(upward_bucket(partial_value), 'gx', split_axis=0, concat_a...  24.8 us
    dot_general x6, matrix products, collect(): jnp.einsum('ejqp,ejq->ejp', permute, shaped, precision=full_precision)  22.3 us
  transfers between devices with their start and end apart: 10, of which 10 were waited for; matrix products, arithmetic and copies ran while one was open for 0% of the time, Pallas kernels for 0%

commit v1 on v0

--- a/solution.py
+++ b/solution.py
@@ -184,14 +184,26 @@
             tiled=True,
         )
         partial_value = apply_blocks(downward_settle(values, fetched))[None]
-        returned = lax.all_to_all(
+        returned = jnp.concatenate(
             lax.all_to_all(
-                upward_bucket(partial_value), "gx", split_axis=0, concat_axis=0, tiled=True
+                jnp.stack(
+                    jnp.split(
+                        lax.all_to_all(
+                            upward_bucket(partial_value),
+                            "gx",
+                            split_axis=0,
+                            concat_axis=0,
+                            tiled=True,
+                        ),
+                        lax.axis_size("gy"),
+                        axis=1,
+                    )
+                ),
+                "gy",
+                0,
+                0,
             ),
-            "gy",
-            split_axis=1,
-            concat_axis=1,
-            tiled=True,
+            axis=1,
         )
         return upward_settle(partial_value, returned)[0]
 

time: 814 us -> 847 us (1.041)
  local copies, waits for them, and re-layouts: 50.7 us -> 84.3 us
    unnamed x26 -> x86, local copies, waits for them, and re-layouts: 5.37 us -> 39.1 us
where the time goes in v1:
time: 847 us; the launch traced here: 837 us
  other arithmetic  352 us (42%)
  blocking collectives  207 us (24%)
  local copies, waits for them, and re-layouts  84.3 us (10%)
  matrix products  79.3 us (9%)
  waiting for transfers between devices  61.4 us (7%)
  starting transfers between devices  38.8 us (5%)
  between operations  15.2 us (2%)
    another operation x4, other arithmetic, condense(): factor = jnp.linalg.cholesky(inner_block)  183 us
    another operation x3, other arithmetic, condense(): solved = jax.scipy.linalg.solve_triangular(factor, coupling, lower=True)  154 us
    psum x4, blocking collectives, pair_total(): lax.psum((owned_dot(residual, precond), owned_dot(precond, mapped)), ('gx...  153 us
    unnamed x86, local copies, waits for them, and re-layouts  39.1 us
    all_to_all x4, blocking collectives, operate(): lax.all_to_all(downward_bucket(values), 'gx', split_axis=0, concat_axis=0...  28.4 us
    all_to_all x4, waiting for transfers between devices, operate(): lax.all_to_all(lax.all_to_all(downward_bucket(values), 'gx', split_axis=0...  25.5 us
    all_to_all x4, waiting for transfers between devices, operate(): lax.all_to_all(jnp.stack(jnp.split(lax.all_to_all(upward_bucket(partial_v...  25.4 us
    all_to_all x4, blocking collectives, operate(): lax.all_to_all(upward_bucket(partial_value), 'gx', split_axis=0, concat_a...  24.8 us
  transfers between devices with their start and end apart: 10, of which 10 were waited for; matrix products, arithmetic and copies ran while one was open for 0% of the time, Pallas kernels for 0%

profile of v1, /device:TPU:0, one launch (start us, length us, event | category | flops | bytes accessed | tf_op | source)
XLA Modules:
  0.0 837.2 jit_solution(12291283799245094013)
XLA Ops:
  1.3 9.7 %fusion = f32[16,275,275]{2,0,1:T(8,128)S(1)} fusion(f32[12,275,275]{2,1,0:T(8,128)} %param.10, f32[16,12]{1,0:T(8,128)S(1)} %copy-done), kind=kOutput, calls=%fused_computation.37 | convolution fusion | flops 174240000 | bytes 8470768 | tf_op jit(solution)/shard_map/while/body/eval_jaxpr/ek,kab->eab/dot_general | solution.py:49
  16.7 183.1 %custom-call.13 = f32[16,125,125]{2,1,0:T(8,128)S(1)} custom-call(f32[16,125,125]{2,1,0:T(8,128)S(1)} %fusion.20), custom_call_target="Cholesky" | custom-call | tf_op jit(solution)/shard_map/while/body/eval_jaxpr/jit(cholesky)/cholesky | solution.py:53
  200.3 154.0 %custom-call.14 = f32[16,1,125,125]{2,3,1,0:T(8,128)S(1)} custom-call(f32[16,1,125,125]{3,2,1,0:T(8,128)S(1)} %select_bitcast_fusion), custom_call_target="InvertDiagBlocksLowerTriangular" | custom-call | tf_op jit(solution)/shard_map/while/body/eval_jaxpr/jit(_solve_triangular)/vmap()/triangular_solve | solution.py:54
  377.6 6.7 copy.725
  406.0 6.4 all-to-all-start.1
  412.5 6.5 all-to-all-done.1
  422.1 6.2 all_to_all.90
  432.6 6.3 all-to-all-done.3
  454.4 6.2 all_to_all.91
  473.2 6.4 all-to-all-done.5
  481.6 38.4 %all-reduce.3 = (f32[]{:T(128)}, f32[]{:T(128)}) all-reduce(f32[]{:T(128)} %get-tuple-element.41, f32[]{:T(128)} %get-tuple-element.40), channel_id=1, replica_groups=mesh['gx'=2,'gy'=16] {'gx','gy'}, use_global_device_ids=true, to_apply=%region_5.6 | all-reduce | flops 2 | bytes 16 | tf_op jit(solution)/shard_map/psum | solution.py:214
  522.7 7.4 all_to_all.92
  534.3 6.4 all-to-all-done.7
  556.5 6.2 all_to_all.93
  575.3 6.4 all-to-all-done.9
  583.7 38.3 %all-reduce.2 = (f32[]{:T(128)}, f32[]{:T(128)}) all-reduce(f32[]{:T(128)} %get-tuple-element.39, f32[]{:T(128)} %get-tuple-element.38), channel_id=1, replica_groups=mesh['gx'=2,'gy'=16] {'gx','gy'}, use_global_device_ids=true, to_apply=%region_13.14 | all-reduce | flops 2 | bytes 16 | tf_op jit(solution)/shard_map/psum | solution.py:214
  627.9 7.4 all_to_all.94
  639.6 6.4 all-to-all-done.11
  680.4 6.4 all-to-all-done.13
  688.8 38.4 %all-reduce.1 = (f32[]{:T(128)}, f32[]{:T(128)}) all-reduce(f32[]{:T(128)} %get-tuple-element.37, f32[]{:T(128)} %get-tuple-element.36), channel_id=1, replica_groups=mesh['gx'=2,'gy'=16] {'gx','gy'}, use_global_device_ids=true, to_apply=%region_21.22 | all-reduce | flops 2 | bytes 16 | tf_op jit(solution)/shard_map/psum | solution.py:214
  732.5 7.4 all_to_all.96
  744.2 6.4 all-to-all-done.15
  785.0 6.4 all-to-all-done.17
  793.5 38.4 %all-reduce = (f32[]{:T(128)}, f32[]{:T(128)}) all-reduce(f32[]{:T(128)} %get-tuple-element.35, f32[]{:T(128)} %get-tuple-element.34), channel_id=1, replica_groups=mesh['gx'=2,'gy'=16] {'gx','gy'}, use_global_device_ids=true, to_apply=%region_29.30 | all-reduce | flops 2 | bytes 16 | tf_op jit(solution)/shard_map/psum | solution.py:214
  (319 shorter events, 210.4 us)
Async XLA Ops:
  0.6 0.7 copy-start
  11.1 2.8 copy-start.2
  354.2 5.9 slice-start
  361.2 5.6 copy-start.4
  361.2 5.9 copy-start.3
  361.2 5.9 copy-start.5
  370.9 2.7 copy-start.1
  370.9 2.6 copy-start.6
  384.2 10.8 %copy-start.8 = (s32[1,2,4]{2,1,0:T(2,128)S(1)}, s32[1,2,4]{2,1,0:T(2,128)}, u32[]{:S(2)}) copy-start(s32[1,2,4]{2,1,0:T(2,128)} %param.15) | copy-start | bytes 100
  384.2 10.9 %copy-start.7 = (s32[1,2,4]{2,1,0:T(2,128)S(1)}, s32[1,2,4]{2,1,0:T(2,128)}, u32[]{:S(2)}) copy-start(s32[1,2,4]{2,1,0:T(2,128)} %param.16) | copy-start | bytes 100
  384.2 11.8 %copy-start.9 = (s32[1,2]{1,0:T(1,128)S(1)}, s32[1,2]{1,0:T(1,128)}, u32[]{:S(2)}) copy-start(s32[1,2]{1,0:T(1,128)} %param.18) | copy-start | bytes 28
  384.2 17.2 %copy-start.10 = (s32[1,2]{1,0:T(1,128)S(1)}, s32[1,2]{1,0:T(1,128)}, u32[]{:S(2)}) copy-start(s32[1,2]{1,0:T(1,128)} %param.17) | copy-start | bytes 28
  397.2 8.2 all-to-all-start
  406.0 13.0 %all-to-all-start.1 = ((f32[2,16,200]{2,0,1:T(2,128)}), f32[2,16,200]{2,0,1:T(2,128)S(1)}, u32[]{:S(2)}, u32[]{:S(2)}) async-start(f32[2,16,200]{2,0,1:T(2,128)} %copy.730), calls=%async_computation.1 | async-start | bytes 65536 | tf_op jit(solution)/shard_map/all_to_all | solution.py:169
  428.9 10.0 %all-to-all-start.3 = ((f32[2,16,100]{2,0,1:T(2,128)}), f32[2,16,100]{2,0,1:T(2,128)S(1)}, u32[]{:S(2)}, u32[]{:S(2)}) async-start(f32[2,16,100]{2,0,1:T(2,128)} %copy.738), calls=%async_computation.3 | async-start | bytes 32768 | tf_op jit(solution)/shard_map/all_to_all | solution.py:179
  469.6 10.0 %all-to-all-start.5 = ((f32[16,2,1,100]{3,1,2,0:T(2,128)}), f32[16,2,1,100]{3,1,2,0:T(2,128)S(1)}, u32[]{:S(2)}, u32[]{:S(2)}) async-start(f32[16,2,1,100]{3,1,2,0:T(2,128)} %constant_dynamic-update-slice_fusion), calls=%async_computation.5 | async-start | bytes 32768 | tf_op jit(solution)/shard_map/all_to_all | solution.py:188
  530.7 10.1 %all-to-all-start.7 = ((f32[2,16,100]{2,0,1:T(2,128)}), f32[2,16,100]{2,0,1:T(2,128)S(1)}, u32[]{:S(2)}, u32[]{:S(2)}) async-start(f32[2,16,100]{2,0,1:T(2,128)} %copy.766), calls=%async_computation.7 | async-start | bytes 32768 | tf_op jit(solution)/shard_map/all_to_all | solution.py:179
  571.7 10.0 %all-to-all-start.9 = ((f32[16,2,1,100]{3,1,2,0:T(2,128)}), f32[16,2,1,100]{3,1,2,0:T(2,128)S(1)}, u32[]{:S(2)}, u32[]{:S(2)}) async-start(f32[16,2,1,100]{3,1,2,0:T(2,128)} %constant_dynamic-update-slice_fusion.16), calls=%async_computation.9 | async-start | bytes 32768 | tf_op jit(solution)/shard_map/all_to_all | solution.py:188
  636.0 10.0 %all-to-all-start.11 = ((f32[2,16,100]{2,0,1:T(2,128)}), f32[2,16,100]{2,0,1:T(2,128)S(1)}, u32[]{:S(2)}, u32[]{:S(2)}) async-start(f32[2,16,100]{2,0,1:T(2,128)} %copy.794), calls=%async_computation.11 | async-start | bytes 32768 | tf_op jit(solution)/shard_map/all_to_all | solution.py:179
  676.8 10.0 %all-to-all-start.13 = ((f32[16,2,1,100]{3,1,2,0:T(2,128)}), f32[16,2,1,100]{3,1,2,0:T(2,128)S(1)}, u32[]{:S(2)}, u32[]{:S(2)}) async-start(f32[16,2,1,100]{3,1,2,0:T(2,128)} %constant_dynamic-update-slice_fusion.32), calls=%async_computation.13 | async-start | bytes 32768 | tf_op jit(solution)/shard_map/all_to_all | solution.py:188
  740.5 10.1 %all-to-all-start.15 = ((f32[2,16,100]{2,0,1:T(2,128)}), f32[2,16,100]{2,0,1:T(2,128)S(1)}, u32[]{:S(2)}, u32[]{:S(2)}) async-start(f32[2,16,100]{2,0,1:T(2,128)} %copy.822), calls=%async_computation.15 | async-start | bytes 32768 | tf_op jit(solution)/shard_map/all_to_all | solution.py:179
  781.4 10.0 %all-to-all-start.17 = ((f32[16,2,1,100]{3,1,2,0:T(2,128)}), f32[16,2,1,100]{3,1,2,0:T(2,128)S(1)}, u32[]{:S(2)}, u32[]{:S(2)}) async-start(f32[16,2,1,100]{3,1,2,0:T(2,128)} %constant_dynamic-update-slice_fusion.48), calls=%async_computation.17 | async-start | bytes 32768 | tf_op jit(solution)/shard_map/all_to_all | solution.py:188
